TPU v7x, 32 devices: a whole 2x2x4 slice. The times are simulated.
32 devices in a mesh: exp: 8 (over z, core), pix: 4 (over y, x).
Axes of the slice: x: 2, y: 2, z: 4, core: 2. Of those that a mesh axis runs over, the one named last changes fastest.
Arguments:
- transmission: bfloat16 [4096, 6144], P('exp', 'pix'), may hold values from 0.29882812 to 1
- inverse_var: bfloat16 [4096, 6144], P('exp', 'pix'), may hold values from 0.25 to 4
- pixel_mask: int32 [4096, 48], P('exp', 'pix'), may hold values 0 or 1
- coef: bfloat16 [4096, 256], P('exp'), may hold values from -6 to 6
- basis: bfloat16 [256, 6144], P(None, 'pix'), may hold values from -6 to 6
- coef_tangent: bfloat16 [4096, 256], P('exp', 'pix'), may hold values from -0.375 to 0.375
- basis_tangent: bfloat16 [256, 6144], P('exp', 'pix'), may hold values from -0.375 to 0.375
Outputs:
- coef_grad: float32 [4096, 256], P('exp', 'pix')
- basis_grad: float32 [256, 6144], P('exp', 'pix')
All inputs are finite; a program needn't handle non-finite values. No bound on the sum of `pixel_mask` on one device may be relied on, other than what follows from the above.
Results may differ from a plain program's by a relative error of at most 0.0008.
Values may be sent and summed in bfloat16 or wider, within the bound.
A program may use at most 64 MiB of HBM per device.

v0:
```python
import functools
import math

import jax
import jax.numpy as jnp
from jax import lax
from jax.experimental import pallas as pl
from jax.experimental.pallas import tpu as pltpu
from jax.sharding import PartitionSpec as P

TILE = 128
WIRE = jnp.int16
TOP = 32767.0
TINY = 1e-30
MESH = pl.DeviceIdType.MESH


def split_columns(cols):
    for pieces in (3, 2):
        if cols % (pieces * TILE) == 0:
            return pieces
    return 1


def scaled(x):
    peak = jnp.maximum(jnp.max(jnp.abs(x), axis=0, keepdims=True), TINY)
    return jnp.round(x * (TOP / peak)).astype(jnp.int32).astype(WIRE), peak * (1.0 / TOP)


def restored(value, factor):
    return value.astype(jnp.int32).astype(jnp.float32) * factor


def kernel(
    n_e, n_p, pieces,
    trans_h, ivar_h, mask_h, coef_h, basis_h, ctan_h, btan_h,
    cout, bout,
    trans, ivar, mask, coef, basis, tg, fb,
    used_rows, used_cols, tang, coef_t, weights, moved, wt,
    part, swap, rs_out, rs_in, rs_fac_out, rs_fac_in,
    cpart, cs_out, cs_in, cs_fac_out, cs_fac_in,
    load_sem, own_sem,
    tg_send, tg_recv, ag_send, ag_recv, near_send, near_recv, fw_send, fw_recv,
    swap_send, swap_recv, rs_send, rs_recv, rsf_send, rsf_recv,
    cs_send, cs_recv, csf_send, csf_recv,
):
    rows, cols = trans.shape
    rank = coef.shape[1]
    width = cols // pieces
    chips = n_e // 2
    cb = rank // n_p
    order = sorted(range(1, chips), key=lambda d: abs(2 * d - chips))
    me_e, me_p = lax.axis_index("exp"), lax.axis_index("pix")
    core, chip = lax.rem(me_e, 2), me_e // 2
    partner = chip * 2 + (1 - core)

    def over(d):
        return lax.rem(chip + d, chips)

    def back(d):
        return lax.rem(chip + chips - d, chips)

    def remote(src, dst, send, recv, e, p):
        return pltpu.make_async_remote_copy(
            src_ref=src, dst_ref=dst, send_sem=send, recv_sem=recv,
            device_id=(e, p), device_id_type=MESH,
        )

    own = []
    for j in range(pieces):
        own.append(pltpu.make_async_copy(
            btan_h.at[:, pl.ds(j * width, width)], fb.at[j, me_e], own_sem.at[j]))
    own.append(pltpu.make_async_copy(ctan_h, tg.at[me_p], own_sem.at[pieces]))
    for copy in own:
        copy.start()
    loads = [
        pltpu.make_async_copy(src, dst, load_sem.at[i])
        for i, (src, dst) in enumerate((
            (trans_h, trans), (ivar_h, ivar), (mask_h, mask), (coef_h, coef), (basis_h, basis)))
    ]
    for copy in loads:
        copy.start()

    barrier = pltpu.get_barrier_semaphore()
    for d in range(1, chips):
        pl.semaphore_signal(barrier, inc=1, device_id=(over(d) * 2 + core, me_p), device_id_type=MESH)
    pl.semaphore_signal(barrier, inc=1, device_id=(partner, me_p), device_id_type=MESH)
    for d in range(1, n_p):
        pl.semaphore_signal(barrier, inc=1, device_id=(me_e, lax.rem(me_p + d, n_p)), device_id_type=MESH)
    pl.semaphore_wait(barrier, chips + n_p - 1)

    sends = []

    def go(copy):
        copy.start()
        sends.append(copy)
        return copy

    gather, near = {}, {}
    for j in range(pieces):
        own[j].wait()
        for d in order:
            gather[j, d] = go(remote(fb.at[j, me_e], fb.at[j, me_e], ag_send.at[j, d], ag_recv.at[j, d],
                                     over(d) * 2 + core, me_p))
        near[j] = go(remote(fb.at[j, me_e], fb.at[j, me_e], near_send.at[j], near_recv.at[j], partner, me_p))
        if j == 0:
            own[pieces].wait()
            tangents = [
                go(remote(tg.at[me_p], tg.at[me_p], tg_send.at[d], tg_recv.at[d],
                          me_e, lax.rem(me_p + d, n_p)))
                for d in range(1, n_p)
            ]

    forwards = {}

    def forward(j):
        for d in order:
            gather[j, d].wait_recv()
            at = back(d) * 2 + core
            forwards[j, d] = go(remote(fb.at[j, at], fb.at[j, at], fw_send.at[j, d], fw_recv.at[j, d],
                                       partner, me_p))

    for copy in loads:
        copy.wait()
    block = TILE

    used_rows[...] = jnp.zeros_like(used_rows)
    used_rows[: mask.shape[0], :] = mask[...].astype(jnp.float32)
    used_cols[...] = used_rows[...].T

    def weigh(r, _):
        at = pl.ds(pl.multiple_of(r * block, block), block)
        used = used_cols[at, :]
        for t in range(cols // TILE):
            here = pl.ds(t * TILE, TILE)
            tr = trans[at, here].astype(jnp.float32)
            weights[at, here] = (
                tr * tr * ivar[at, here].astype(jnp.float32)
                * jnp.broadcast_to(used[:, t:t + 1], (block, TILE)))
        return 0

    lax.fori_loop(0, rows // block, weigh, 0)
    coef_t[...] = coef[...].T

    for copy in tangents:
        copy.wait_recv()
    tang[...] = tg[...].reshape(rank, rows).T

    def first_term(r, _):
        at = pl.ds(pl.multiple_of(r * block, block), block)
        for j in range(pieces):
            here = pl.ds(j * width, width)
            moved[at, here] = jnp.dot(tang[at, :], basis[:, here], preferred_element_type=jnp.float32)
        return 0

    lax.fori_loop(0, rows // block, first_term, 0)

    def work(j):
        here = pl.ds(j * width, width)
        near[j].wait_recv()
        for d in range(1, chips):
            forwards[j, d].wait_recv()
        full = fb[j].reshape(rank, width)

        def second_term(r, _):
            at = pl.ds(pl.multiple_of(r * block, block), block)
            total = moved[at, here] + jnp.dot(coef[at, :], full, preferred_element_type=jnp.float32)
            wt[at, :] = (weights[at, here] * total).astype(jnp.bfloat16)
            return 0

        lax.fori_loop(0, rows // block, second_term, 0)
        term = jnp.dot(coef_t[...], wt[...], preferred_element_type=jnp.float32)
        part[j] = term.reshape(chips, 2, rank // n_e, width)
        copy = go(remote(part.at[j, :, 1 - core], swap.at[j], swap_send.at[j], swap_recv.at[j], partner, me_p))
        cterm = lax.dot_general(
            basis[:, here], wt[...], (((1,), (1,)), ((), ())), preferred_element_type=jnp.float32
        ).reshape(n_p, cb, rows)
        cpart[...] = cterm if j == 0 else cpart[...] + cterm
        return copy

    def scatter(j, copy):
        copy.wait_recv()
        out = []
        for d in range(1, chips):
            to = over(d)
            value, factor = scaled(part[j, to, core] + swap[j, to])
            rs_out[j, d] = value
            rs_fac_out[j, d] = factor
            out.append(go(remote(rs_out.at[j, d], rs_in.at[j, d], rs_send.at[j, d], rs_recv.at[j, d],
                                 to * 2 + core, me_p)))
            out.append(go(remote(rs_fac_out.at[j, d], rs_fac_in.at[j, d], rsf_send.at[j, d], rsf_recv.at[j, d],
                                 to * 2 + core, me_p)))
        return out

    swaps, scatters = {}, {}
    forward(0)
    for j in range(pieces):
        swaps[j] = work(j)
        if j + 1 < pieces:
            forward(j + 1)
        else:
            csent = []
            for d in range(1, n_p):
                to = lax.rem(me_p + d, n_p)
                value, factor = scaled(cpart[to])
                cs_out[d] = value
                cs_fac_out[d] = factor
                csent.append(go(remote(cs_out.at[d], cs_in.at[d], cs_send.at[d], cs_recv.at[d], me_e, to)))
                csent.append(go(remote(cs_fac_out.at[d], cs_fac_in.at[d], csf_send.at[d], csf_recv.at[d], me_e, to)))
        scatters[j] = scatter(j, swaps[j])

    for copy in csent:
        copy.wait_recv()
    total = cpart[me_p]
    for d in range(1, n_p):
        total = total + restored(cs_in[d], cs_fac_in[d])
    cout[...] = total

    for j in range(pieces):
        for copy in scatters[j]:
            copy.wait_recv()
        total = part[j, chip, core] + swap[j, chip]
        for d in range(1, chips):
            total = total + restored(rs_in[j, d], rs_fac_in[j, d])
        bout[:, j * width:(j + 1) * width] = total

    for copy in sends:
        copy.wait_send()


def finish(by_pixels, by_exposures, coef_sum, basis_sum, coef_grad, basis_grad):
    coef_grad[...] = coef_sum[...] * by_pixels
    basis_grad[...] = basis_sum[...] * by_exposures


def body(n_e, n_p, *args):
    trans, ivar, mask, coef, basis, ctan, btan = args
    rows, cols = trans.shape
    rank = coef.shape[1]
    chips = n_e // 2
    rb, cb = rank // n_e, rank // n_p
    pieces = split_columns(cols)
    width = cols // pieces
    padded = -(-mask.shape[1] // TILE) * TILE
    f32, bf16 = jnp.float32, jnp.bfloat16
    dma = pltpu.SemaphoreType.DMA
    V = pltpu.VMEM
    coef_sum, basis_sum = pl.pallas_call(
        functools.partial(kernel, n_e, n_p, pieces),
        out_shape=(jax.ShapeDtypeStruct((cb, rows), f32), jax.ShapeDtypeStruct((rb, cols), f32)),
        in_specs=[pl.BlockSpec(memory_space=pl.ANY)] * 7,
        out_specs=(pl.BlockSpec(memory_space=pltpu.VMEM),) * 2,
        scratch_shapes=[
            V(trans.shape, bf16), V(ivar.shape, bf16), V(mask.shape[::-1], jnp.int32), V(coef.shape, bf16),
            V(basis.shape, bf16), V((n_p, cb, rows), bf16), V((pieces, n_e, rb, width), bf16),
            V((padded, rows), f32), V((rows, padded), f32),
            V((rows, rank), bf16), V((rank, rows), bf16), V((rows, cols), f32), V((rows, cols), f32),
            V((rows, width), bf16),
            V((pieces, chips, 2, rb, width), f32), V((pieces, chips, rb, width), f32),
            V((pieces, chips, rb, width), WIRE), V((pieces, chips, rb, width), WIRE),
            V((pieces, chips, 1, width), f32), V((pieces, chips, 1, width), f32),
            V((n_p, cb, rows), f32), V((n_p, cb, rows), WIRE), V((n_p, cb, rows), WIRE),
            V((n_p, 1, rows), f32), V((n_p, 1, rows), f32),
            dma((5,)), dma((pieces + 1,)),
            dma((n_p,)), dma((n_p,)), dma((pieces, chips)), dma((pieces, chips)),
            dma((pieces,)), dma((pieces,)), dma((pieces, chips)), dma((pieces, chips)),
            dma((pieces,)), dma((pieces,)), dma((pieces, chips)), dma((pieces, chips)),
            dma((pieces, chips)), dma((pieces, chips)),
            dma((n_p,)), dma((n_p,)), dma((n_p,)), dma((n_p,)),
        ],
        compiler_params=pltpu.CompilerParams(
            collective_id=0, has_side_effects=True, vmem_limit_bytes=56 * 1024 * 1024
        ),
    )(trans, ivar, mask.T, coef, basis, ctan.T, btan)
    coef_grad, basis_grad = pl.pallas_call(
        functools.partial(finish, 1.0 / math.sqrt(cols * n_p), 1.0 / math.sqrt(rows * n_e)),
        out_shape=(jax.ShapeDtypeStruct((cb, rows), f32), jax.ShapeDtypeStruct((rb, cols), f32)),
    )(coef_sum, basis_sum)
    return coef_grad.T, basis_grad


def solution(mesh):
    placed = (
        P("exp", "pix"),
        P("exp", "pix"),
        P("exp", "pix"),
        P("exp", None),
        P(None, "pix"),
        P("exp", "pix"),
        P("exp", "pix"),
    )
    return jax.shard_map(
        functools.partial(body, mesh.shape["exp"], mesh.shape["pix"]),
        mesh=mesh,
        in_specs=placed,
        out_specs=(P("exp", "pix"), P("exp", "pix")),
        check_vma=False,
    )
```

profile of v0, /device:TPU:0, one launch (start us, length us, event | category | flops | bytes accessed | tf_op | source)
XLA Modules:
  0.0 29.8 jit_solution(13268028340896412509)
XLA Ops:
  0.6 27.5 %shard_map.86 = (f32[64,512]{1,0:T(8,128)}, f32[32,1536]{1,0:T(8,128)}) custom-call(bf16[512,1536]{1,0:T(8,128)(2,1)} %trans_h.1, bf16[512,1536]{1,0:T(8,128)(2,1)} %ivar_h.1, s32[12,512]{1,0:T(8,128)} %bitcast.4, bf16[512,256]{1,0:T(8,128)(2,1)} %coef_h.1, bf16[256,1536]{1,0:T(8,128)(2,1)} %basis_h.1, bf16[64,512]{1,0:T(8,128)(2,1)} %bitcast.3, ...), custom_call_target="tpu_custom_call" | custom-call | tf_op jit(solution)/shard_map/pallas_call | solution.py:248
  28.1 1.7 %shard_map.87 = (f32[64,512]{1,0:T(8,128)}, f32[32,1536]{1,0:T(8,128)}) custom-call(f32[64,512]{1,0:T(8,128)} %get-tuple-element.6.coef_sum, f32[32,1536]{1,0:T(8,128)} %get-tuple-element.7.basis_sum), custom_call_target="tpu_custom_call" | custom-call | tf_op jit(solution)/shard_map/pallas_call | solution.py:275
where the time goes:
time: 30 us; the launch traced here: 29.8 us
  Pallas kernels  29.2 us (97%)
  between operations  0.64 us (2%)
    pallas_call x1, Pallas kernels, body(): pl.pallas_call(functools.partial(kernel, n_e, n_p, pieces), out_shape=(ja...  27.5 us
    pallas_call x1, Pallas kernels, body(): pl.pallas_call(functools.partial(finish, 1.0 / math.sqrt(cols * n_p), 1.0...  1.74 us

commit v1 on v0

--- a/solution.py
+++ b/solution.py
@@ -214,7 +214,7 @@
     total = cpart[me_p]
     for d in range(1, n_p):
         total = total + restored(cs_in[d], cs_fac_in[d])
-    cout[...] = total
+    cout[...] = total * (1.0 / math.sqrt(cols * n_p))
 
     for j in range(pieces):
         for copy in scatters[j]:
@@ -222,7 +222,7 @@
         total = part[j, chip, core] + swap[j, chip]
         for d in range(1, chips):
             total = total + restored(rs_in[j, d], rs_fac_in[j, d])
-        bout[:, j * width:(j + 1) * width] = total
+        bout[:, j * width:(j + 1) * width] = total * (1.0 / math.sqrt(rows * n_e))
 
     for copy in sends:
         copy.wait_send()
@@ -231,6 +231,15 @@
 def finish(by_pixels, by_exposures, coef_sum, basis_sum, coef_grad, basis_grad):
     coef_grad[...] = coef_sum[...] * by_pixels
     basis_grad[...] = basis_sum[...] * by_exposures
+
+
+def drain(a, b, x, y, sem):
+    c0 = pltpu.make_async_copy(a, x, sem.at[0])
+    c1 = pltpu.make_async_copy(b, y, sem.at[1])
+    c1.start()
+    c0.start()
+    c1.wait()
+    c0.wait()
 
 
 def body(n_e, n_p, *args):
@@ -247,7 +256,7 @@
     V = pltpu.VMEM
     coef_sum, basis_sum = pl.pallas_call(
         functools.partial(kernel, n_e, n_p, pieces),
-        out_shape=(jax.ShapeDtypeStruct((cb, rows), f32), jax.ShapeDtypeStruct((rb, cols), f32)),
+        out_shape=(pltpu.VMEM((cb, rows), f32), pltpu.VMEM((rb, cols), f32)),
         in_specs=[pl.BlockSpec(memory_space=pl.ANY)] * 7,
         out_specs=(pl.BlockSpec(memory_space=pltpu.VMEM),) * 2,
         scratch_shapes=[
@@ -273,9 +282,12 @@
         ),
     )(trans, ivar, mask.T, coef, basis, ctan.T, btan)
     coef_grad, basis_grad = pl.pallas_call(
-        functools.partial(finish, 1.0 / math.sqrt(cols * n_p), 1.0 / math.sqrt(rows * n_e)),
+        drain,
         out_shape=(jax.ShapeDtypeStruct((cb, rows), f32), jax.ShapeDtypeStruct((rb, cols), f32)),
-    )(coef_sum, basis_sum)
+        in_specs=[pl.BlockSpec(memory_space=pltpu.VMEM)] * 2,
+        out_specs=(pl.BlockSpec(memory_space=pl.ANY),) * 2,
+        scratch_shapes=[dma((2,))],
+    )(pltpu.with_memory_space_constraint(coef_sum, pltpu.VMEM), pltpu.with_memory_space_constraint(basis_sum, pltpu.VMEM))
     return coef_grad.T, basis_grad
 
 

time: 30 us -> 28.3 us (0.943)
  Pallas kernels: 29.2 us -> 27.5 us
    pallas_call x2, Pallas kernels: 29.2 us -> 27.5 us  [the longest x1 26.8 us: body(): pl.pallas_call(functools.partial(kernel, n_e, n_p, pieces), out_shape=(pl...]
where the time goes in v1:
time: 28.3 us; the launch traced here: 28.1 us
  Pallas kernels  27.5 us (97%)
  between operations  0.64 us (2%)
    pallas_call x1, Pallas kernels, body(): pl.pallas_call(functools.partial(kernel, n_e, n_p, pieces), out_shape=(pl...  26.8 us
    pallas_call x1, Pallas kernels, body(): pl.pallas_call(drain, out_shape=(jax.ShapeDtypeStruct((cb, rows), f32), j...  0.74 us

profile of v1, /device:TPU:0, one launch (start us, length us, event | category | flops | bytes accessed | tf_op | source)
XLA Modules:
  0.0 28.1 jit_solution(10545106983873663526)
XLA Ops:
  0.6 26.8 %shard_map.86 = (f32[64,512]{1,0:T(8,128)S(1)}, f32[32,1536]{1,0:T(8,128)S(1)}) custom-call(bf16[512,1536]{1,0:T(8,128)(2,1)} %trans_h.1, bf16[512,1536]{1,0:T(8,128)(2,1)} %ivar_h.1, s32[12,512]{1,0:T(8,128)} %bitcast.4, bf16[512,256]{1,0:T(8,128)(2,1)} %coef_h.1, bf16[256,1536]{1,0:T(8,128)(2,1)} %basis_h.1, bf16[64,512]{1,0:T(8,128)(2,1)} %bitcast.3, ...), custom_call_target="tpu_custom_call" | custom-call | tf_op jit(solution)/shard_map/pallas_call | solution.py:257
  27.4 0.7 %shard_map.87 = (f32[64,512]{1,0:T(8,128)}, f32[32,1536]{1,0:T(8,128)}) custom-call(f32[64,512]{1,0:T(8,128)S(1)} %get-tuple-element.6.a, f32[32,1536]{1,0:T(8,128)S(1)} %get-tuple-element.7.b), custom_call_target="tpu_custom_call" | custom-call | tf_op jit(solution)/shard_map/pallas_call | solution.py:284

commit v2 on v1

v2 whole, which is shorter than its diff:
```python
import functools
import math

import jax
import jax.numpy as jnp
from jax import lax
from jax.experimental import pallas as pl
from jax.experimental.pallas import tpu as pltpu
from jax.sharding import PartitionSpec as P

TILE = 128
WIRE = jnp.int16
PIECES = 2
TOP = 32767.0
TINY = 1e-30
MESH = pl.DeviceIdType.MESH


def split_columns(cols):
    tiles = cols // (2 * TILE)
    pieces = min(PIECES, tiles)
    return [TILE * ((tiles + i) // pieces) for i in reversed(range(pieces))]


def scaled(x):
    peak = jnp.maximum(jnp.max(jnp.abs(x), axis=0, keepdims=True), TINY)
    return jnp.round(x * (TOP / peak)).astype(jnp.int32).astype(WIRE), peak * (1.0 / TOP)


def restored(value, factor):
    return value.astype(jnp.int32).astype(jnp.float32) * factor


def kernel(n_e, n_p, widths, trans_h, ivar_h, mask_h, coef_h, basis_h, ctan_h, btan_h, cout, bout, *scratch):
    scratch = list(scratch)

    def take(n=None):
        if n is None:
            return scratch.pop(0)
        return [scratch.pop(0) for _ in range(n)]

    pieces = len(widths)
    trans, ivar, mask, coef, basis, tg = take(6)
    fb, bo = take(pieces), take(pieces)
    used_rows, used_cols, tang, coef_t, weights, moved = take(6)
    wt, part, pin, rs_out, rs_in, rs_fac_out, rs_fac_in = (take(pieces) for _ in range(7))
    cpart, cswap, cs_out, cs_in, cs_fac_out, cs_fac_in = take(6)
    load_sem, own_sem, far_sem = take(3)
    tg_send, tg_recv, ag_send, ag_recv, fw_send, ex_send, ex_recv = take(7)
    pin_send, pin_recv, rs_send, rs_recv, rsf_send, rsf_recv = take(6)
    sw_send, sw_recv, cs_send, cs_recv, csf_send, csf_recv = take(6)
    assert not scratch
    rows, half = trans.shape[1:]
    rank = coef.shape[2]
    starts = [sum(widths[:j]) for j in range(pieces)]
    chips = n_e // 2
    cb = rank // n_p
    me_e, me_p = lax.axis_index("exp"), lax.axis_index("pix")
    core, chip = lax.rem(me_e, 2), me_e // 2
    across = 1 - core
    partner = chip * 2 + across

    def lanes(c, start, width):
        return pl.ds(pl.multiple_of(c * half + start, TILE), width)

    def remote(src, dst, send, recv, e, p):
        return pltpu.make_async_remote_copy(
            src_ref=src, dst_ref=dst, send_sem=send, recv_sem=recv,
            device_id=(e, p), device_id_type=MESH,
        )

    own, far = [], []
    for j in range(pieces):
        own.append(pltpu.make_async_copy(
            btan_h.at[:, lanes(core, starts[j], widths[j])], fb[j].at[chip, core], own_sem.at[j]))
        far.append(pltpu.make_async_copy(
            btan_h.at[:, lanes(across, starts[j], widths[j])], bo[j], far_sem.at[j]))
    own.append(pltpu.make_async_copy(ctan_h, tg.at[core, me_p], own_sem.at[pieces]))
    for copy in own[:pieces] + far + own[pieces:]:
        copy.start()
    mine = lanes(core, 0, half)
    loads = [
        pltpu.make_async_copy(src, dst, load_sem.at[i])
        for i, (src, dst) in enumerate((
            (trans_h.at[:, mine], trans.at[core]), (ivar_h.at[:, mine], ivar.at[core]), (mask_h, mask.at[core]),
            (coef_h, coef.at[core]), (basis_h.at[:, mine], basis)))
    ]
    for copy in loads:
        copy.start()

    barrier = pltpu.get_barrier_semaphore()
    for d in range(1, chips):
        for c in range(2):
            pl.semaphore_signal(barrier, inc=1, device_id=(lax.rem(chip + d, chips) * 2 + c, me_p), device_id_type=MESH)
    pl.semaphore_signal(barrier, inc=1, device_id=(partner, me_p), device_id_type=MESH)
    for d in range(1, n_p):
        pl.semaphore_signal(barrier, inc=1, device_id=(me_e, lax.rem(me_p + d, n_p)), device_id_type=MESH)
    pl.semaphore_wait(barrier, 2 * (chips - 1) + n_p)

    sends = []

    def go(copy):
        copy.start()
        sends.append(copy)
        return copy

    hub = chips == 4
    if hub:
        side = chip // 2
        end, inner = 3 * side, 1 + side
        far_end, far_inner = 3 - end, 3 - inner
        is_inner = chip == inner
        mate = jnp.where(is_inner, end, inner)
        targets = [far_inner, mate]
    else:
        targets = [lax.rem(chip + d, chips) for d in range(1, chips)]

    def send_own(j):
        mine, theirs = fb[j].at[chip, core], bo[j]
        for i, to in enumerate(targets):
            go(remote(mine, mine, ag_send.at[j, i, 0], ag_recv.at[j, chip, core], to * 2 + core, me_p))
            go(remote(theirs, mine, ag_send.at[j, i, 1], ag_recv.at[j, chip, core], to * 2 + across, me_p))
        go(remote(theirs, mine, ag_send.at[j, chips - 1, 1], ag_recv.at[j, chip, core], partner, me_p))

    def arrived(j, k, c):
        block = fb[j].at[k, c]
        remote(block, block, ag_send.at[j, 0, 0], ag_recv.at[j, k, c], partner, me_p).wait_recv()

    def pass_copy(j, i):
        k = (far_inner, far_end)[i]
        return remote(fb[j].at[k], fb[j].at[k], fw_send.at[j, i], ag_recv.at[j, k, 0], end * 2 + core, me_p)

    def pass_on(j):
        if not hub:
            return

        @pl.when(is_inner)
        def _():
            for i in range(2):
                k = (far_inner, far_end)[i]
                arrived(j, k, 0)
                arrived(j, k, 1)
                pass_copy(j, i).start()

    def complete(j):
        arrived(j, chip, across)
        if not hub:
            for to in targets:
                arrived(j, to, 0)
                arrived(j, to, 1)
            return
        arrived(j, mate, 0)
        arrived(j, mate, 1)

        @pl.when(jnp.logical_not(is_inner))
        def _():
            pass_copy(j, 0).wait_recv()
            pass_copy(j, 1).wait_recv()

    for j in range(pieces):
        own[j].wait()
        far[j].wait()
        send_own(j)
    own[pieces].wait()
    tangents = [
        go(remote(tg.at[core, me_p], tg.at[core, me_p], tg_send.at[d], tg_recv.at[d],
                  me_e, lax.rem(me_p + d, n_p)))
        for d in range(1, n_p)
    ]
    theirs = lanes(across, 0, half)
    exchanged = [
        go(remote(src, dst, ex_send.at[i], ex_recv.at[i], partner, me_p))
        for i, (src, dst) in enumerate((
            (mask_h, mask.at[core]), (coef_h, coef.at[core]),
            (trans_h.at[:, theirs], trans.at[core]), (ivar_h.at[:, theirs], ivar.at[core])))
    ]
    block = TILE
    tiles = half // TILE
    used_rows[...] = jnp.zeros_like(used_rows)

    def weigh_all(c):
        used = mask[c].astype(jnp.float32)
        used_rows[c, :tiles, :] = jnp.where(core == 0, used[:tiles], used[tiles:])
        used_cols[c] = used_rows[c].T

        def weigh(r, _):
            at = pl.ds(pl.multiple_of(r * block, block), block)
            used = used_cols[c, at, :]
            for t in range(tiles):
                here = pl.ds(t * TILE, TILE)
                tr = trans[c, at, here].astype(jnp.float32)
                weights[c, at, here] = (
                    tr * tr * ivar[c, at, here].astype(jnp.float32)
                    * jnp.broadcast_to(used[:, t:t + 1], (block, TILE)))
            return 0

        lax.fori_loop(0, rows // block, weigh, 0)
        coef_t[c] = coef[c].T


    def first(c):
        tang[c] = tg[c].reshape(rank, rows).T

        def first_term(r, _):
            at = pl.ds(pl.multiple_of(r * block, block), block)
            for j in range(pieces):
                here = pl.ds(starts[j], widths[j])
                moved[c, at, here] = jnp.dot(tang[c, at, :], basis[:, here], preferred_element_type=jnp.float32)
            return 0

        lax.fori_loop(0, rows // block, first_term, 0)

    for copy in loads:
        copy.wait()
    weigh_all(core)
    pass_on(0)
    for copy in tangents:
        copy.wait_recv()
    other_tangent = go(remote(tg.at[core], tg.at[core], ex_send.at[4], ex_recv.at[4], partner, me_p))
    first(core)
    for j in range(1, pieces):
        pass_on(j)
    for copy in exchanged:
        copy.wait_recv()
    weigh_all(across)
    other_tangent.wait_recv()
    first(across)

    def other(i, me):
        return i + (i >= me).astype(jnp.int32)

    def slot_at(to, me):
        return jnp.where(me > to, me - 1, me)

    def swap_copy(to):
        return remote(cpart.at[across, to], cswap.at[to], sw_send.at[to], sw_recv.at[to], partner, me_p)

    def work(j):
        width = widths[j]
        here = pl.ds(starts[j], width)
        complete(j)
        full = fb[j][...].reshape(rank, width)
        for c in range(2):
            total = moved[c, :, here] + jnp.dot(coef[c], full, preferred_element_type=jnp.float32)
            wt[j][c] = (weights[c, :, here] * total).astype(jnp.bfloat16)

        def coef_part():
            for c in range(2):
                cterm = lax.dot_general(
                    basis[:, here], wt[j][c], (((1,), (1,)), ((), ())), preferred_element_type=jnp.float32
                ).reshape(n_p, cb, rows)
                cpart[c] = cterm if j == 0 else cpart[c] + cterm

        last = j + 1 == pieces
        if last:
            coef_part()
            for i in range(n_p - 1):
                swap_copy(other(i, me_p)).start()
            swap_copy(me_p).start()
        term = (jnp.dot(coef_t[0], wt[j][0], preferred_element_type=jnp.float32)
                + jnp.dot(coef_t[1], wt[j][1], preferred_element_type=jnp.float32))
        part[j][...] = term.reshape(chips, 2, rank // n_e, width)
        scatter(j)
        if not last:
            coef_part()

    def rs_copies(j, i, c, to, slot, at):
        return (remote(rs_out[j].at[i, c], rs_in[j].at[slot, at], rs_send.at[j, i, c], rs_recv.at[j, slot, at],
                       to * 2 + c, me_p),
                remote(rs_fac_out[j].at[i, c], rs_fac_in[j].at[slot, at], rsf_send.at[j, i, c], rsf_recv.at[j, slot, at],
                       to * 2 + c, me_p))

    def scatter(j):
        for i in range(chips - 1):
            to = other(i, chip)
            slot = slot_at(to, chip)
            for c in range(2):
                value, factor = scaled(part[j][to, c])
                rs_out[j][i, c] = value
                rs_fac_out[j][i, c] = factor
                for copy in rs_copies(j, i, c, to, slot, core):
                    go(copy)
        go(remote(part[j].at[chip, across], pin[j], pin_send.at[j], pin_recv.at[j], partner, me_p))

    def gathered(j):
        remote(pin[j], pin[j], pin_send.at[j], pin_recv.at[j], partner, me_p).wait_recv()
        totals = [jnp.where(core == h, part[j][chip, core], pin[j][...]) for h in range(2)]
        for i in range(chips - 1):
            for h in range(2):
                for copy in rs_copies(j, i, 0, chip, i, h):
                    copy.wait_recv()
                totals[h] = totals[h] + restored(rs_in[j][i, h], rs_fac_in[j][i, h])
        for h in range(2):
            at = h * half + starts[j]
            bout[:, at:at + widths[j]] = totals[h] * (1.0 / math.sqrt(rows * n_e))

    for j in range(pieces):
        work(j)

    for i in range(n_p - 1):
        to = other(i, me_p)
        slot = slot_at(to, me_p)
        swap_copy(to).wait_recv()
        value, factor = scaled(cpart[core, to] + cswap[to])
        cs_out[i] = value
        cs_fac_out[i] = factor
        go(remote(cs_out.at[i], cs_in.at[slot], cs_send.at[i], cs_recv.at[slot], me_e, to))
        go(remote(cs_fac_out.at[i], cs_fac_in.at[slot], csf_send.at[i], csf_recv.at[slot], me_e, to))
    swap_copy(me_p).wait_recv()

    for j in range(pieces - 1):
        gathered(j)
    gathered(pieces - 1)
    total = cpart[core, me_p] + cswap[me_p]
    for i in range(n_p - 1):
        remote(cs_out.at[i], cs_in.at[i], cs_send.at[i], cs_recv.at[i], partner, me_p).wait_recv()
        remote(cs_fac_out.at[i], cs_fac_in.at[i], csf_send.at[i], csf_recv.at[i], partner, me_p).wait_recv()
        total = total + restored(cs_in[i], cs_fac_in[i])
    cout[...] = total * (1.0 / math.sqrt(half * 2 * n_p))

    for copy in sends:
        copy.wait_send()
    for i in range(n_p):
        swap_copy(i).wait_send()
    if hub:
        @pl.when(is_inner)
        def _():
            for j in range(pieces):
                pass_copy(j, 0).wait_send()
                pass_copy(j, 1).wait_send()


def drain(a, b, x, y, sem):
    c0 = pltpu.make_async_copy(a, x, sem.at[0])
    c1 = pltpu.make_async_copy(b, y, sem.at[1])
    c1.start()
    c0.start()
    c1.wait()
    c0.wait()


def body(n_e, n_p, *args):
    trans, ivar, mask, coef, basis, ctan, btan = args
    rows, cols = trans.shape
    rank = coef.shape[1]
    chips = n_e // 2
    rb, cb = rank // n_e, rank // n_p
    widths = split_columns(cols)
    pieces = len(widths)
    half = cols // 2
    padded = -(-(half // TILE) // TILE) * TILE
    f32, bf16 = jnp.float32, jnp.bfloat16
    dma = pltpu.SemaphoreType.DMA
    V = pltpu.VMEM

    def each(shape, dtype):
        return [V(tuple(w if v is None else v for v in shape), dtype) for w in widths]

    coef_sum, basis_sum = pl.pallas_call(
        functools.partial(kernel, n_e, n_p, widths),
        out_shape=(pltpu.VMEM((cb, rows), f32), pltpu.VMEM((rb, cols), f32)),
        in_specs=[pl.BlockSpec(memory_space=pl.ANY)] * 7,
        out_specs=(pl.BlockSpec(memory_space=pltpu.VMEM),) * 2,
        scratch_shapes=[
            V((2, rows, half), bf16), V((2, rows, half), bf16), V((2, *mask.shape[::-1]), jnp.int32),
            V((2, rows, rank), bf16), V((rank, half), bf16), V((2, n_p, cb, rows), bf16),
            *each((chips, 2, rb, None), bf16), *each((rb, None), bf16),
            V((2, padded, rows), f32), V((2, rows, padded), f32),
            V((2, rows, rank), bf16), V((2, rank, rows), bf16), V((2, rows, half), f32), V((2, rows, half), f32),
            *each((2, rows, None), bf16),
            *each((chips, 2, rb, None), f32), *each((rb, None), f32),
            *each((chips - 1, 2, rb, None), WIRE), *each((chips - 1, 2, rb, None), WIRE),
            *each((chips - 1, 2, 1, None), f32), *each((chips - 1, 2, 1, None), f32),
            V((2, n_p, cb, rows), f32), V((n_p, cb, rows), f32), V((n_p, cb, rows), WIRE), V((n_p, cb, rows), WIRE),
            V((n_p, 1, rows), f32), V((n_p, 1, rows), f32),
            dma((5,)), dma((pieces + 1,)), dma((pieces,)),
            dma((n_p,)), dma((n_p,)), dma((pieces, chips, 2)), dma((pieces, chips, 2)), dma((pieces, 2)),
            dma((5,)), dma((5,)),
            dma((pieces,)), dma((pieces,)), dma((pieces, chips, 2)), dma((pieces, chips, 2)),
            dma((pieces, chips, 2)), dma((pieces, chips, 2)),
            dma((n_p,)), dma((n_p,)), dma((n_p,)), dma((n_p,)), dma((n_p,)), dma((n_p,)),
        ],
        compiler_params=pltpu.CompilerParams(
            collective_id=0, has_side_effects=True, vmem_limit_bytes=56 * 1024 * 1024
        ),
    )(trans, ivar, mask.T, coef, basis, ctan.T, btan)
    coef_grad, basis_grad = pl.pallas_call(
        drain,
        out_shape=(jax.ShapeDtypeStruct((cb, rows), f32), jax.ShapeDtypeStruct((rb, cols), f32)),
        in_specs=[pl.BlockSpec(memory_space=pltpu.VMEM)] * 2,
        out_specs=(pl.BlockSpec(memory_space=pl.ANY),) * 2,
        scratch_shapes=[dma((2,))],
    )(*[pltpu.with_memory_space_constraint(v, pltpu.VMEM) for v in (coef_sum, basis_sum)])
    return coef_grad.T, basis_grad


def solution(mesh):
    placed = (
        P("exp", "pix"),
        P("exp", "pix"),
        P("exp", "pix"),
        P("exp", None),
        P(None, "pix"),
        P("exp", "pix"),
        P("exp", "pix"),
    )
    return jax.shard_map(
        functools.partial(body, mesh.shape["exp"], mesh.shape["pix"]),
        mesh=mesh,
        in_specs=placed,
        out_specs=(P("exp", "pix"), P("exp", "pix")),
        check_vma=False,
    )
```

time: 28.3 us -> 27 us (0.954)
  Pallas kernels: 27.5 us -> 26.2 us
    pallas_call x1, Pallas kernels: 26.8 us -> 25.5 us  [body(): pl.pallas_call(functools.partial(kernel, n_e, n_p, widths), out_shape=(pl...]
where the time goes in v2:
time: 27 us; the launch traced here: 26.9 us
  Pallas kernels  26.2 us (97%)
  between operations  0.64 us (2%)
    pallas_call x1, Pallas kernels, body(): pl.pallas_call(functools.partial(kernel, n_e, n_p, widths), out_shape=(pl...  25.5 us
    pallas_call x1, Pallas kernels, body(): pl.pallas_call(drain, out_shape=(jax.ShapeDtypeStruct((cb, rows), f32), j...  0.74 us

profile of v2, /device:TPU:0, one launch (start us, length us, event | category | flops | bytes accessed | tf_op | source)
XLA Modules:
  0.0 26.9 jit_solution(2420557001801668066)
XLA Ops:
  0.6 25.5 %shard_map.86 = (f32[64,512]{1,0:T(8,128)S(1)}, f32[32,1536]{1,0:T(8,128)S(1)}) custom-call(bf16[512,1536]{1,0:T(8,128)(2,1)} %trans_h.1, bf16[512,1536]{1,0:T(8,128)(2,1)} %ivar_h.1, s32[12,512]{1,0:T(8,128)} %bitcast.4, bf16[512,256]{1,0:T(8,128)(2,1)} %coef_h.1, bf16[256,1536]{1,0:T(8,128)(2,1)} %basis_h.1, bf16[64,512]{1,0:T(8,128)(2,1)} %bitcast.3, ...), custom_call_target="tpu_custom_call" | custom-call | tf_op jit(solution)/shard_map/pallas_call | solution.py:359
  26.1 0.7 %shard_map.87 = (f32[64,512]{1,0:T(8,128)}, f32[32,1536]{1,0:T(8,128)}) custom-call(f32[64,512]{1,0:T(8,128)S(1)} %get-tuple-element.6.a, f32[32,1536]{1,0:T(8,128)S(1)} %get-tuple-element.7.b), custom_call_target="tpu_custom_call" | custom-call | tf_op jit(solution)/shard_map/pallas_call | solution.py:387

commit v3 on v2

--- a/solution.py
+++ b/solution.py
@@ -10,16 +10,14 @@
 
 TILE = 128
 WIRE = jnp.int16
-PIECES = 2
 TOP = 32767.0
 TINY = 1e-30
 MESH = pl.DeviceIdType.MESH
 
-
 def split_columns(cols):
     tiles = cols // (2 * TILE)
-    pieces = min(PIECES, tiles)
-    return [TILE * ((tiles + i) // pieces) for i in reversed(range(pieces))]
+    first = tiles // 3
+    return [TILE * v for v in (first, tiles - first) if v]
 
 
 def scaled(x):
@@ -115,12 +113,16 @@
     else:
         targets = [lax.rem(chip + d, chips) for d in range(1, chips)]
 
+    def send_to(j, i, to):
+        mine, theirs = fb[j].at[chip, core], bo[j]
+        return (remote(mine, mine, ag_send.at[j, i, 0], ag_recv.at[j, chip, core], to * 2 + core, me_p),
+                remote(theirs, mine, ag_send.at[j, i, 1], ag_recv.at[j, chip, core], to * 2 + across, me_p))
+
     def send_own(j):
-        mine, theirs = fb[j].at[chip, core], bo[j]
         for i, to in enumerate(targets):
-            go(remote(mine, mine, ag_send.at[j, i, 0], ag_recv.at[j, chip, core], to * 2 + core, me_p))
-            go(remote(theirs, mine, ag_send.at[j, i, 1], ag_recv.at[j, chip, core], to * 2 + across, me_p))
-        go(remote(theirs, mine, ag_send.at[j, chips - 1, 1], ag_recv.at[j, chip, core], partner, me_p))
+            for copy in send_to(j, i, to):
+                go(copy)
+        go(remote(bo[j], fb[j].at[chip, core], ag_send.at[j, chips - 1, 1], ag_recv.at[j, chip, core], partner, me_p))
 
     def arrived(j, k, c):
         block = fb[j].at[k, c]
@@ -154,8 +156,8 @@
 
         @pl.when(jnp.logical_not(is_inner))
         def _():
-            pass_copy(j, 0).wait_recv()
-            pass_copy(j, 1).wait_recv()
+            for i in range(2):
+                pass_copy(j, i).wait_recv()
 
     for j in range(pieces):
         own[j].wait()
@@ -197,7 +199,6 @@
         lax.fori_loop(0, rows // block, weigh, 0)
         coef_t[c] = coef[c].T
 
-
     def first(c):
         tang[c] = tg[c].reshape(rank, rows).T
 
@@ -235,34 +236,51 @@
     def swap_copy(to):
         return remote(cpart.at[across, to], cswap.at[to], sw_send.at[to], sw_recv.at[to], partner, me_p)
 
+    def start_swap():
+        for i in range(n_p - 1):
+            swap_copy(other(i, me_p)).start()
+        swap_copy(me_p).start()
+
     def work(j):
         width = widths[j]
         here = pl.ds(starts[j], width)
+        last = j + 1 == pieces
         complete(j)
         full = fb[j][...].reshape(rank, width)
-        for c in range(2):
+
+        def second(c):
             total = moved[c, :, here] + jnp.dot(coef[c], full, preferred_element_type=jnp.float32)
             wt[j][c] = (weights[c, :, here] * total).astype(jnp.bfloat16)
 
-        def coef_part():
-            for c in range(2):
-                cterm = lax.dot_general(
-                    basis[:, here], wt[j][c], (((1,), (1,)), ((), ())), preferred_element_type=jnp.float32
-                ).reshape(n_p, cb, rows)
-                cpart[c] = cterm if j == 0 else cpart[c] + cterm
-
-        last = j + 1 == pieces
+        def coef_part(c):
+            cterm = lax.dot_general(
+                basis[:, here], wt[j][c], (((1,), (1,)), ((), ())), preferred_element_type=jnp.float32
+            ).reshape(n_p, cb, rows)
+            cpart[c] = cterm if j == 0 else cpart[c] + cterm
+
         if last:
-            coef_part()
-            for i in range(n_p - 1):
-                swap_copy(other(i, me_p)).start()
-            swap_copy(me_p).start()
+            second(across)
+            coef_part(across)
+            start_swap()
+            second(core)
+        else:
+            second(0)
+            second(1)
         term = (jnp.dot(coef_t[0], wt[j][0], preferred_element_type=jnp.float32)
                 + jnp.dot(coef_t[1], wt[j][1], preferred_element_type=jnp.float32))
         part[j][...] = term.reshape(chips, 2, rank // n_e, width)
         scatter(j)
         if not last:
-            coef_part()
+            coef_part(0)
+            coef_part(1)
+        else:
+            coef_part(core)
+
+    def rs_joint(j, i, to, slot):
+        return (remote(rs_out[j].at[i], rs_in[j].at[slot], rs_send.at[j, i, 0], rs_recv.at[j, slot, 0],
+                       to * 2 + core, me_p),
+                remote(rs_fac_out[j].at[i], rs_fac_in[j].at[slot], rsf_send.at[j, i, 0], rsf_recv.at[j, slot, 0],
+                       to * 2 + core, me_p))
 
     def rs_copies(j, i, c, to, slot, at):
         return (remote(rs_out[j].at[i, c], rs_in[j].at[slot, at], rs_send.at[j, i, c], rs_recv.at[j, slot, at],
@@ -270,22 +288,45 @@
                 remote(rs_fac_out[j].at[i, c], rs_fac_in[j].at[slot, at], rsf_send.at[j, i, c], rsf_recv.at[j, slot, at],
                        to * 2 + c, me_p))
 
+    merged = [j + 1 < pieces for j in range(pieces)]
+
+    def put(j, i, c, total):
+        value, factor = scaled(total)
+        rs_out[j][i, c] = value
+        rs_fac_out[j][i, c] = factor
+
     def scatter(j):
         for i in range(chips - 1):
             to = other(i, chip)
             slot = slot_at(to, chip)
             for c in range(2):
-                value, factor = scaled(part[j][to, c])
-                rs_out[j][i, c] = value
-                rs_fac_out[j][i, c] = factor
-                for copy in rs_copies(j, i, c, to, slot, core):
+                put(j, i, c, part[j][to, c])
+                if not merged[j]:
+                    for copy in rs_copies(j, i, c, to, slot, core):
+                        go(copy)
+            if merged[j]:
+                for copy in rs_joint(j, i, to, slot):
                     go(copy)
+        if not merged[j]:
+            go(remote(part[j].at[chip, across], pin[j], pin_send.at[j], pin_recv.at[j], partner, me_p))
+
+    def reduced(j):
+        if not merged[j]:
+            return
+        totals = [part[j][chip, c] for c in range(2)]
+        for i in range(chips - 1):
+            for copy in rs_joint(j, i, chip, i):
+                copy.wait_recv()
+            for c in range(2):
+                totals[c] = totals[c] + restored(rs_in[j][i, c], rs_fac_in[j][i, c])
+        for c in range(2):
+            part[j][chip, c] = totals[c]
         go(remote(part[j].at[chip, across], pin[j], pin_send.at[j], pin_recv.at[j], partner, me_p))
 
     def gathered(j):
         remote(pin[j], pin[j], pin_send.at[j], pin_recv.at[j], partner, me_p).wait_recv()
         totals = [jnp.where(core == h, part[j][chip, core], pin[j][...]) for h in range(2)]
-        for i in range(chips - 1):
+        for i in range(0 if merged[j] else chips - 1):
             for h in range(2):
                 for copy in rs_copies(j, i, 0, chip, i, h):
                     copy.wait_recv()
@@ -308,9 +349,10 @@
         go(remote(cs_fac_out.at[i], cs_fac_in.at[slot], csf_send.at[i], csf_recv.at[slot], me_e, to))
     swap_copy(me_p).wait_recv()
 
-    for j in range(pieces - 1):
+    for j in range(pieces):
+        reduced(j)
+    for j in range(pieces):
         gathered(j)
-    gathered(pieces - 1)
     total = cpart[core, me_p] + cswap[me_p]
     for i in range(n_p - 1):
         remote(cs_out.at[i], cs_in.at[i], cs_send.at[i], cs_recv.at[i], partner, me_p).wait_recv()
@@ -326,8 +368,8 @@
         @pl.when(is_inner)
         def _():
             for j in range(pieces):
-                pass_copy(j, 0).wait_send()
-                pass_copy(j, 1).wait_send()
+                for i in range(2):
+                    pass_copy(j, i).wait_send()
 
 
 def drain(a, b, x, y, sem):

time: 27 us -> 25.8 us (0.956)
  Pallas kernels: 26.2 us -> 25 us
    pallas_call x1, Pallas kernels: 25.5 us -> 24.2 us  [body(): pl.pallas_call(functools.partial(kernel, n_e, n_p, widths), out_shape=(pl...]
where the time goes in v3:
time: 25.8 us; the launch traced here: 25.6 us
  Pallas kernels  25 us (97%)
  between operations  0.64 us (2%)
    pallas_call x1, Pallas kernels, body(): pl.pallas_call(functools.partial(kernel, n_e, n_p, widths), out_shape=(pl...  24.2 us
    pallas_call x1, Pallas kernels, body(): pl.pallas_call(drain, out_shape=(jax.ShapeDtypeStruct((cb, rows), f32), j...  0.74 us

profile of v3, /device:TPU:0, one launch (start us, length us, event | category | flops | bytes accessed | tf_op | source)
XLA Modules:
  0.0 25.6 jit_solution(12775526713022636932)
XLA Ops:
  0.6 24.2 %shard_map.86 = (f32[64,512]{1,0:T(8,128)S(1)}, f32[32,1536]{1,0:T(8,128)S(1)}) custom-call(bf16[512,1536]{1,0:T(8,128)(2,1)} %trans_h.1, bf16[512,1536]{1,0:T(8,128)(2,1)} %ivar_h.1, s32[12,512]{1,0:T(8,128)} %bitcast.4, bf16[512,256]{1,0:T(8,128)(2,1)} %coef_h.1, bf16[256,1536]{1,0:T(8,128)(2,1)} %basis_h.1, bf16[64,512]{1,0:T(8,128)(2,1)} %bitcast.3, ...), custom_call_target="tpu_custom_call" | custom-call | tf_op jit(solution)/shard_map/pallas_call | solution.py:401
  24.9 0.7 %shard_map.87 = (f32[64,512]{1,0:T(8,128)}, f32[32,1536]{1,0:T(8,128)}) custom-call(f32[64,512]{1,0:T(8,128)S(1)} %get-tuple-element.6.a, f32[32,1536]{1,0:T(8,128)S(1)} %get-tuple-element.7.b), custom_call_target="tpu_custom_call" | custom-call | tf_op jit(solution)/shard_map/pallas_call | solution.py:429

commit v4 on v3

--- a/solution.py
+++ b/solution.py
@@ -163,12 +163,13 @@
         own[j].wait()
         far[j].wait()
         send_own(j)
-    own[pieces].wait()
-    tangents = [
-        go(remote(tg.at[core, me_p], tg.at[core, me_p], tg_send.at[d], tg_recv.at[d],
-                  me_e, lax.rem(me_p + d, n_p)))
-        for d in range(1, n_p)
-    ]
+        if j == 0:
+            own[pieces].wait()
+            tangents = [
+                go(remote(tg.at[core, me_p], tg.at[core, me_p], tg_send.at[d], tg_recv.at[d],
+                          me_e, lax.rem(me_p + d, n_p)))
+                for d in range(1, n_p)
+            ]
     theirs = lanes(across, 0, half)
     exchanged = [
         go(remote(src, dst, ex_send.at[i], ex_recv.at[i], partner, me_p))
@@ -246,6 +247,8 @@
         here = pl.ds(starts[j], width)
         last = j + 1 == pieces
         complete(j)
+        if j:
+            release(j - 1)
         full = fb[j][...].reshape(rank, width)
 
         def second(c):
@@ -270,11 +273,10 @@
                 + jnp.dot(coef_t[1], wt[j][1], preferred_element_type=jnp.float32))
         part[j][...] = term.reshape(chips, 2, rank // n_e, width)
         scatter(j)
+        own_rows(j)
         if not last:
             coef_part(0)
-            coef_part(1)
-        else:
-            coef_part(core)
+        coef_part(1 if not last else core)
 
     def rs_joint(j, i, to, slot):
         return (remote(rs_out[j].at[i], rs_in[j].at[slot], rs_send.at[j, i, 0], rs_recv.at[j, slot, 0],
@@ -295,18 +297,26 @@
         rs_out[j][i, c] = value
         rs_fac_out[j][i, c] = factor
 
+    def ship(j, i):
+        to = other(i, chip)
+        slot = slot_at(to, chip)
+        for c in range(2):
+            put(j, i, c, part[j][to, c])
+            if not merged[j]:
+                for copy in rs_copies(j, i, c, to, slot, core):
+                    go(copy)
+
+    def release(j):
+        for i in range(chips - 1):
+            to = other(i, chip)
+            for copy in rs_joint(j, i, to, slot_at(to, chip)):
+                go(copy)
+
     def scatter(j):
         for i in range(chips - 1):
-            to = other(i, chip)
-            slot = slot_at(to, chip)
-            for c in range(2):
-                put(j, i, c, part[j][to, c])
-                if not merged[j]:
-                    for copy in rs_copies(j, i, c, to, slot, core):
-                        go(copy)
-            if merged[j]:
-                for copy in rs_joint(j, i, to, slot):
-                    go(copy)
+            ship(j, i)
+
+    def own_rows(j):
         if not merged[j]:
             go(remote(part[j].at[chip, across], pin[j], pin_send.at[j], pin_recv.at[j], partner, me_p))
 

time: 25.8 us -> 25.6 us (level)
  no operation moved by 1% of the time
where the time goes in v4:
time: 25.6 us; the launch traced here: 25.5 us
  Pallas kernels  24.8 us (97%)
  between operations  0.64 us (2%)
    pallas_call x1, Pallas kernels, body(): pl.pallas_call(functools.partial(kernel, n_e, n_p, widths), out_shape=(pl...  24.1 us
    pallas_call x1, Pallas kernels, body(): pl.pallas_call(drain, out_shape=(jax.ShapeDtypeStruct((cb, rows), f32), j...  0.74 us

profile of v4, /device:TPU:0, one launch (start us, length us, event | category | flops | bytes accessed | tf_op | source)
XLA Modules:
  0.0 25.5 jit_solution(3480053148924276085)
XLA Ops:
  0.6 24.1 %shard_map.86 = (f32[64,512]{1,0:T(8,128)S(1)}, f32[32,1536]{1,0:T(8,128)S(1)}) custom-call(bf16[512,1536]{1,0:T(8,128)(2,1)} %trans_h.1, bf16[512,1536]{1,0:T(8,128)(2,1)} %ivar_h.1, s32[12,512]{1,0:T(8,128)} %bitcast.4, bf16[512,256]{1,0:T(8,128)(2,1)} %coef_h.1, bf16[256,1536]{1,0:T(8,128)(2,1)} %basis_h.1, bf16[64,512]{1,0:T(8,128)(2,1)} %bitcast.3, ...), custom_call_target="tpu_custom_call" | custom-call | tf_op jit(solution)/shard_map/pallas_call | solution.py:411
  24.7 0.7 %shard_map.87 = (f32[64,512]{1,0:T(8,128)}, f32[32,1536]{1,0:T(8,128)}) custom-call(f32[64,512]{1,0:T(8,128)S(1)} %get-tuple-element.6.a, f32[32,1536]{1,0:T(8,128)S(1)} %get-tuple-element.7.b), custom_call_target="tpu_custom_call" | custom-call | tf_op jit(solution)/shard_map/pallas_call | solution.py:439

commit v5 on v4

--- a/solution.py
+++ b/solution.py
@@ -198,7 +198,6 @@
             return 0
 
         lax.fori_loop(0, rows // block, weigh, 0)
-        coef_t[c] = coef[c].T
 
     def first(c):
         tang[c] = tg[c].reshape(rank, rows).T
@@ -227,6 +226,8 @@
     weigh_all(across)
     other_tangent.wait_recv()
     first(across)
+    for c in range(2):
+        coef_t[c] = coef[c].T
 
     def other(i, me):
         return i + (i >= me).astype(jnp.int32)

time: 25.6 us -> 25.7 us (level)
  no operation moved by 1% of the time
where the time goes in v5:
time: 25.7 us; the launch traced here: 25.4 us
  Pallas kernels  24.8 us (96%)
  between operations  0.64 us (2%)
    pallas_call x1, Pallas kernels, body(): pl.pallas_call(functools.partial(kernel, n_e, n_p, widths), out_shape=(pl...  24 us
    pallas_call x1, Pallas kernels, body(): pl.pallas_call(drain, out_shape=(jax.ShapeDtypeStruct((cb, rows), f32), j...  0.74 us

profile of v5, /device:TPU:0, one launch (start us, length us, event | category | flops | bytes accessed | tf_op | source)
XLA Modules:
  0.0 25.4 jit_solution(16790798300291701740)
XLA Ops:
  0.6 24.0 %shard_map.86 = (f32[64,512]{1,0:T(8,128)S(1)}, f32[32,1536]{1,0:T(8,128)S(1)}) custom-call(bf16[512,1536]{1,0:T(8,128)(2,1)} %trans_h.1, bf16[512,1536]{1,0:T(8,128)(2,1)} %ivar_h.1, s32[12,512]{1,0:T(8,128)} %bitcast.4, bf16[512,256]{1,0:T(8,128)(2,1)} %coef_h.1, bf16[256,1536]{1,0:T(8,128)(2,1)} %basis_h.1, bf16[64,512]{1,0:T(8,128)(2,1)} %bitcast.3, ...), custom_call_target="tpu_custom_call" | custom-call | tf_op jit(solution)/shard_map/pallas_call | solution.py:412
  24.7 0.7 %shard_map.87 = (f32[64,512]{1,0:T(8,128)}, f32[32,1536]{1,0:T(8,128)}) custom-call(f32[64,512]{1,0:T(8,128)S(1)} %get-tuple-element.6.a, f32[32,1536]{1,0:T(8,128)S(1)} %get-tuple-element.7.b), custom_call_target="tpu_custom_call" | custom-call | tf_op jit(solution)/shard_map/pallas_call | solution.py:440
